TPU v7x, 32 devices: a 4x4x1 block of a 4x4x8 slice. The times are simulated.
32 devices in a mesh: rep: 1 (over z), r: 4 (over y), s: 8 (over x, core).
Axes of the slice: x: 4, y: 4, z: 1, core: 2. Of those that a mesh axis runs over, the one named last changes fastest.
The devices are a block of a 4x4x8 slice.
Arguments:
- x: bfloat16 [32, 2048, 1024], P(('rep', 'r', 's'))
- dy: bfloat16 [32, 2048, 1024], P(('rep', 'r', 's'))
- w_gate: bfloat16 [2, 1024, 2560], P(None, 's')
- w_up: bfloat16 [2, 1024, 2560], P(None, 's')
- w_down: bfloat16 [2, 2560, 1024], P(None, 's')
- m_w_gate: float32 [2, 1024, 2560], P(None, 's')
- m_w_up: float32 [2, 1024, 2560], P(None, 's')
- m_w_down: float32 [2, 2560, 1024], P(None, 's')
- v_w_gate: float32 [2, 1024, 2560], P(None, 's')
- v_w_up: float32 [2, 1024, 2560], P(None, 's')
- v_w_down: float32 [2, 2560, 1024], P(None, 's')
Outputs:
- output 1: bfloat16 [2, 1024, 2560], P('rep', 's')
- output 2: bfloat16 [2, 1024, 2560], P('rep', 's')
- output 3: bfloat16 [2, 2560, 1024], P('rep', 's')
- output 4: float32 [2, 1024, 2560], P('rep', 's')
- output 5: float32 [2, 1024, 2560], P('rep', 's')
- output 6: float32 [2, 2560, 1024], P('rep', 's')
- output 7: float32 [2, 1024, 2560], P('rep', 's')
- output 8: float32 [2, 1024, 2560], P('rep', 's')
- output 9: float32 [2, 2560, 1024], P('rep', 's')
All inputs are finite; a program needn't handle non-finite values.
Results may differ from a plain program's by a relative error of at most 0.022.
Values are sent between devices in bfloat16 or wider.
A program may use at most 768 MiB of HBM per device.

v0:
```python
import jax
import jax.numpy as jnp
from jax import lax
from jax.sharding import PartitionSpec as P

NAMES = ("w_gate", "w_up", "w_down")


def matmul(a, w):
    return jnp.dot(a, w, preferred_element_type=jnp.float32).astype(jnp.bfloat16)


def normed(h):
    wide = h.astype(jnp.float32)
    scale = lax.rsqrt(jnp.mean(wide**2, -1, keepdims=True) + 1e-6)
    return (wide * scale).astype(jnp.bfloat16)


def layer(h, w):
    a = normed(h)
    gate = jnp.dot(a, w["w_gate"], preferred_element_type=jnp.float32)
    up = jnp.dot(a, w["w_up"], preferred_element_type=jnp.float32)
    return h + matmul((jax.nn.silu(gate) * up).astype(jnp.bfloat16), w["w_down"])


def adamw(w, m, v, g):
    m = 0.9 * m + 0.1 * g
    v = 0.95 * v + 0.05 * g * g
    step = m * lax.rsqrt(v + 1e-8) + 0.1 * w
    return (w - 0.02 * step).astype(jnp.bfloat16), m, v


def clipped(gradients, sum_of_squares, count):
    factor = jnp.minimum(1.0, 0.5 * lax.rsqrt(sum_of_squares / count + 1e-30))
    return [g * factor for g in gradients]


def solution(mesh):
    def fetched(weights, number):
        return {name: lax.all_gather(w[number], "s", axis=0, tiled=True) for name, w in zip(NAMES, weights, strict=True)}

    def summed(term):
        return lax.psum(lax.psum_scatter(term, "s", scatter_dimension=0, tiled=True), "r")

    def step(x, dy, *arrays):
        weights, m, v = (arrays[i : i + 3] for i in (0, 3, 6))
        layers = weights[0].shape[0]
        h, kept = x[0], []
        for number in range(layers):
            kept.append(h)
            h = layer(h, fetched(weights, number))
        by_h, mine = dy[0], [None] * layers
        for number in reversed(range(layers)):
            _, back = jax.vjp(lambda w, h: layer(h, w), fetched(weights, number), kept[number])
            by_w, by_h = back(by_h)
            mine[number] = [summed(by_w[name]) for name in NAMES]
        gradients = [jnp.stack([mine[number][i] for number in range(layers)]).astype(jnp.float32) for i in range(3)]
        squares = lax.psum(sum(jnp.sum(g * g) for g in gradients), "s")
        gradients = clipped(gradients, squares, lax.psum(1, "s") * sum(g.size for g in gradients))
        new = [adamw(w.astype(jnp.float32), m, v, g) for w, m, v, g in zip(weights, m, v, gradients, strict=True)]
        return tuple(one[which] for which in range(3) for one in new)

    states, cut = P(("rep", "r", "s"), None, None), P(None, "s", None)
    return jax.shard_map(
        step,
        mesh=mesh,
        in_specs=(states, states) + (cut,) * 9,
        out_specs=(P("rep", "s", None),) * 9,
        check_vma=False,
    )
```

profile of v0, /device:TPU:96, one launch (start us, length us, event | category | flops | bytes accessed | tf_op | source)
XLA Modules:
  0.0 683.5 jit_solution(9085730194788429331)
XLA Ops:
  15.7 6.5 copy.20
  22.2 3.1 fusion.15
  25.3 6.5 copy.21
  31.8 14.6 %all-gather.13.cloned.1.call-done = bf16[1,1024,2560]{2,1,0:T(8,128)(2,1)} async-done(((bf16[1,128,2560]{2,1,0:T(8,128)(2,1)}), bf16[1,1024,2560]{2,1,0:T(8,128)(2,1)}) %all-gather.13.cloned.1.call-update) | async-done | bytes 5242896 | tf_op jit(solution)/shard_map/all_gather | solution.py:40
  46.4 18.4 %fusion.41 = f32[2048,2560]{1,0:T(8,128)} fusion(bf16[1,1024,2560]{2,1,0:T(8,128)(2,1)} %all-gather.13.cloned.1.call-done, bf16[1,2048,1024]{1,2,0:T(8,128)(2,1)} %copy.20, f32[2048]{0:T(1024)S(1)} %add_rsqrt_fusion), kind=kOutput, calls=%fused_computation.59 | convolution fusion | flops 10743709696 | bytes 30416896 | tf_op jit(solution)/shard_map/dot_general | solution.py:21
  64.7 17.5 %all-gather.15.cloned.1.call-done = bf16[1,1024,2560]{2,1,0:T(8,128)(2,1)} async-done(((bf16[1,128,2560]{2,1,0:T(8,128)(2,1)}), bf16[1,1024,2560]{2,1,0:T(8,128)(2,1)}) %all-gather.15.cloned.1.call-update) | async-done | bytes 5242896 | tf_op jit(solution)/shard_map/all_gather | solution.py:40
  82.3 28.6 %multiply_convert_fusion.1 = (bf16[2048,2560]{1,0:T(8,128)(2,1)}, f32[2048,2560]{1,0:T(8,128)}) fusion(f32[2048,2560]{1,0:T(8,128)} %fusion.41, bf16[1,1024,2560]{2,1,0:T(8,128)(2,1)} %all-gather.15.cloned.1.call-done, bf16[1,2048,1024]{1,2,0:T(8,128)(2,1)} %copy.20, f32[2048]{0:T(1024)S(1)} %add_rsqrt_fusion), kind=kOutput, calls=%fused_computation.17 | convolution fusion | flops 10775166976 | bytes 61874176 | tf_op jit(solution)/shard_map/dot_general | solution.py:22
  110.8 7.3 %all-gather.17.cloned.1.call-done = bf16[1,2560,1024]{2,1,0:T(8,128)(2,1)} async-done(((bf16[1,320,1024]{2,1,0:T(8,128)(2,1)}), bf16[1,2560,1024]{2,1,0:T(8,128)(2,1)}) %all-gather.17.cloned.1.call-update) | async-done | bytes 5242896 | tf_op jit(solution)/shard_map/all_gather | solution.py:40
  118.2 17.8 %fusion.19 = (f32[2048]{0:T(1024)S(1)}, bf16[2048,1024]{0,1:T(8,128)(2,1)}) fusion(bf16[2048,2560]{1,0:T(8,128)(2,1)} %get-tuple-element.30, bf16[1,2560,1024]{2,1,0:T(8,128)(2,1)} %all-gather.17.cloned.1.call-done, bf16[1,2048,1024]{1,2,0:T(8,128)(2,1)} %copy.20), kind=kOutput, calls=%fused_computation.37 | convolution fusion | flops 10747901952 | bytes 24125440 | tf_op jit(solution)/shard_map/dot_general | solution.py:10
  136.6 17.3 %all-gather.21.cloned.1.call-done = bf16[1,2560,1024]{2,1,0:T(8,128)(2,1)} async-done(((bf16[1,320,1024]{2,1,0:T(8,128)(2,1)}), bf16[1,2560,1024]{2,1,0:T(8,128)(2,1)}) %all-gather.21.cloned.1.call-update) | async-done | bytes 5242896 | tf_op jit(solution)/shard_map/all_gather | solution.py:40
  153.9 17.2 %convolution_convert_fusion.1 = bf16[2048,2560]{1,0:T(8,128)(2,1)} fusion(bf16[1,2560,1024]{2,1,0:T(8,128)(2,1)} %all-gather.21.cloned.1.call-done, bf16[1,2048,1024]{2,1,0:T(8,128)(2,1)} %param.12), kind=kOutput, calls=%fused_computation.27 | convolution fusion | flops 10742661120 | bytes 19922944 | tf_op jit(solution)/shard_map/transpose(jvp())/dot_general | solution.py:10
  171.1 18.6 %all-gather.23.cloned.1.call-done = bf16[1,1024,2560]{2,1,0:T(8,128)(2,1)} async-done(((bf16[1,128,2560]{2,1,0:T(8,128)(2,1)}), bf16[1,1024,2560]{2,1,0:T(8,128)(2,1)}) %all-gather.23.cloned.1.call-update) | async-done | bytes 5242896 | tf_op jit(solution)/shard_map/all_gather | solution.py:40
  189.7 18.3 %fusion.28 = f32[2048,2560]{1,0:T(8,128)} fusion(bf16[1,1024,2560]{2,1,0:T(8,128)(2,1)} %all-gather.23.cloned.1.call-done, bf16[2048,1024]{0,1:T(8,128)(2,1)} %get-tuple-element.33, f32[2048]{0:T(1024)S(1)} %fusion.80), kind=kOutput, calls=%fused_computation.46 | convolution fusion | flops 10743709696 | bytes 30416896 | tf_op jit(solution)/shard_map/jvp()/dot_general | solution.py:22
  207.9 17.5 %all-gather.19.cloned.1.call-done = bf16[1,1024,2560]{2,1,0:T(8,128)(2,1)} async-done(((bf16[1,128,2560]{2,1,0:T(8,128)(2,1)}), bf16[1,1024,2560]{2,1,0:T(8,128)(2,1)}) %all-gather.19.cloned.1.call-update) | async-done | bytes 5242896 | tf_op jit(solution)/shard_map/all_gather | solution.py:40
  225.4 32.2 %fusion.2 = (bf16[2048,2560]{1,0:T(8,128)(2,1)}, f32[2048,2560]{1,0:T(8,128)}) fusion(f32[2048,2560]{1,0:T(8,128)} %fusion.28, bf16[2048,2560]{1,0:T(8,128)(2,1)} %convolution_convert_fusion.1, bf16[1,1024,2560]{2,1,0:T(8,128)(2,1)} %all-gather.19.cloned.1.call-done, bf16[2048,1024]{0,1:T(8,128)(2,1)} %get-tuple-element.33, f32[2048]{0:T(1024)S(1)} %fusion.80), kind=kOutput, calls=%fused_computation.8 | convolution fusion | flops 10806624256 | bytes 72359936 | tf_op jit(solution)/shard_map/jvp()/dot_general | solution.py:21
  257.6 20.0 %fusion.12 = bf16[2048,1024]{0,1:T(8,128)(2,1)} fusion(bf16[2048,2560]{1,0:T(8,128)(2,1)} %convolution_convert_fusion.1, bf16[1,1024,2560]{2,1,0:T(8,128)(2,1)} %all-gather.23.cloned.1.call-done, f32[2048,2560]{1,0:T(8,128)} %get-tuple-element.35), kind=kOutput, calls=%fused_computation.25 | convolution fusion | flops 10768875520 | bytes 40894464 | tf_op jit(solution)/shard_map/transpose(jvp())/dot_general | solution.py:22
  277.7 17.5 %fusion.21 = (f32[2048]{0:T(1024)S(1)}, bf16[2048,1024]{0,1:T(8,128)(2,1)S(1)}) fusion(bf16[2048,1024]{0,1:T(8,128)(2,1)} %get-tuple-element.33, bf16[2048,1024]{0,1:T(8,128)(2,1)} %fusion.12, bf16[2048,2560]{1,0:T(8,128)(2,1)} %get-tuple-element.34, bf16[1,1024,2560]{2,1,0:T(8,128)(2,1)} %all-gather.19.cloned.1.call-done), kind=kOutput, calls=%fused_computation.39 | convolution fusion | flops 10747901952 | bytes 28319744 | tf_op jit(solution)/shard_map/transpose(jvp())/dot_general | solution.py:21
  295.2 3.6 fusion.43
  300.8 15.9 %convolution_convert_fusion.2 = bf16[2560,1024]{1,0:T(8,128)(2,1)} fusion(bf16[2048,2560]{1,0:T(8,128)(2,1)} %get-tuple-element.30, bf16[2048,1024]{0,1:T(8,128)(2,1)S(1)} %fusion.43), kind=kOutput, calls=%fused_computation.44 | convolution fusion | flops 10740039680 | bytes 19922944 | tf_op jit(solution)/shard_map/transpose(jvp())/dot_general | solution.py:10
  316.8 21.9 %fusion.22 = bf16[2560,1024]{1,0:T(8,128)(2,1)} fusion(f32[2048,2560]{1,0:T(8,128)} %fusion.28, bf16[1,2048,1024]{2,1,0:T(8,128)(2,1)} %param.12, f32[2048,2560]{1,0:T(8,128)} %get-tuple-element.35), kind=kOutput, calls=%fused_computation.40 | convolution fusion | flops 10771496960 | bytes 51380224 | tf_op jit(solution)/shard_map/transpose(jvp())/dot_general | solution.py:10
  338.8 17.1 %convolution_convert_fusion = bf16[2048,2560]{1,0:T(8,128)(2,1)} fusion(bf16[2048,1024]{0,1:T(8,128)(2,1)} %copy-done.6, bf16[1,2560,1024]{2,1,0:T(8,128)(2,1)} %all-gather.17.cloned.1.call-done), kind=kOutput, calls=%fused_computation.26 | convolution fusion | flops 10742661120 | bytes 19922944 | tf_op jit(solution)/shard_map/transpose(jvp())/dot_general | solution.py:10
  355.9 20.2 %fusion.27 = bf16[1024,2560]{1,0:T(8,128)(2,1)} fusion(bf16[2048,2560]{1,0:T(8,128)(2,1)} %convolution_convert_fusion, f32[2048,2560]{1,0:T(8,128)} %fusion.41, bf16[1,2048,1024]{1,2,0:T(8,128)(2,1)} %copy.20, f32[2048]{0:T(1024)S(1)} %copy-done.20), kind=kOutput, calls=%fused_computation.43 | convolution fusion | flops 10777788416 | bytes 40902656 | tf_op jit(solution)/shard_map/transpose(jvp())/dot_general | solution.py:22
  376.9 20.2 %fusion.23 = bf16[1024,2560]{1,0:T(8,128)(2,1)} fusion(bf16[2048,2560]{1,0:T(8,128)(2,1)} %convolution_convert_fusion.1, bf16[2048,1024]{0,1:T(8,128)(2,1)} %get-tuple-element.33, f32[2048]{0:T(1024)S(1)} %copy-done.16, f32[2048,2560]{1,0:T(8,128)} %get-tuple-element.35), kind=kOutput, calls=%fused_computation.41 | convolution fusion | flops 10777788416 | bytes 40902656 | tf_op jit(solution)/shard_map/transpose(jvp())/dot_general | solution.py:22
  397.2 25.1 %fusion.24 = bf16[1024,2560]{1,0:T(8,128)(2,1)} fusion(f32[2048,2560]{1,0:T(8,128)} %fusion.41, f32[2048,2560]{1,0:T(8,128)} %get-tuple-element.31, bf16[2048,2560]{1,0:T(8,128)(2,1)} %convolution_convert_fusion, bf16[1,2048,1024]{1,2,0:T(8,128)(2,1)} %copy.20, f32[2048]{0:T(1024)S(1)} %copy-done.20), kind=kOutput, calls=%fused_computation.42 | convolution fusion | flops 10804002816 | bytes 61874176 | tf_op jit(solution)/shard_map/transpose(jvp())/dot_general | solution.py:21
  422.5 16.8 %convolution_convert_fusion.3 = bf16[1024,2560]{1,0:T(8,128)(2,1)} fusion(bf16[2048,2560]{1,0:T(8,128)(2,1)} %get-tuple-element.34, bf16[2048,1024]{0,1:T(8,128)(2,1)} %get-tuple-element.33, f32[2048]{0:T(1024)S(1)} %copy-done.16), kind=kOutput, calls=%fused_computation.45 | convolution fusion | flops 10743709696 | bytes 19931136 | tf_op jit(solution)/shard_map/transpose(jvp())/dot_general | solution.py:21
  439.5 32.5 %reduce-scatter.13.cloned.1.call-done = bf16[128,2560]{1,0:T(8,128)(2,1)} async-done(((bf16[1024,2560]{1,0:T(8,128)(2,1)}), bf16[128,2560]{1,0:T(8,128)(2,1)}) %reduce-scatter.13.cloned.1.call-update) | async-done | bytes 655376 | tf_op jit(solution)/shard_map/reduce_scatter | solution.py:43
  471.9 39.2 %reduce-scatter.7.cloned.1.call-done = bf16[128,2560]{1,0:T(8,128)(2,1)} async-done(((bf16[1024,2560]{1,0:T(8,128)(2,1)}), bf16[128,2560]{1,0:T(8,128)(2,1)}) %reduce-scatter.7.cloned.1.call-update) | async-done | bytes 655376 | tf_op jit(solution)/shard_map/reduce_scatter | solution.py:43
  511.1 39.0 %reduce-scatter.9.cloned.1.call-done = bf16[128,2560]{1,0:T(8,128)(2,1)} async-done(((bf16[1024,2560]{1,0:T(8,128)(2,1)}), bf16[128,2560]{1,0:T(8,128)(2,1)}) %reduce-scatter.9.cloned.1.call-update) | async-done | bytes 655376 | tf_op jit(solution)/shard_map/reduce_scatter | solution.py:43
  550.2 85.4 %all-reduce.3.cloned.1.call-done = (bf16[1,128,2560]{2,1,0:T(8,128)(2,1)}, bf16[1,128,2560]{2,1,0:T(8,128)(2,1)}, bf16[1,128,2560]{2,1,0:T(8,128)(2,1)}, bf16[1,...) async-done(((bf16[1,128,2560]{2,1,0:T(8,128)(2,1)}, bf16[1,128,2560]{2,1,0:T(8,128)(2,1)}, bf16[1,128,2560]{2,1,0:T(8,128)(2,1)}, ...) | async-done | bytes 3932176 | tf_op jit(solution)/shard_map/psum | solution.py:43
  645.4 14.8 %psum.55 = f32[]{:T(128)} all-reduce(f32[]{:T(128)S(6)} %add.111), channel_id=1, replica_groups=mesh['rep'=1,'r'=4,'s'=8] {'s'}, use_global_device_ids=true, to_apply=%region_18.19 | all-reduce | flops 1 | bytes 8 | tf_op jit(solution)/shard_map/psum | solution.py:58
  661.0 6.1 fusion.76
  670.3 6.2 fusion.67
  (80 shorter events, 23.3 us)
Async XLA Ops:
  7.2 5.3 copy-start.1
  7.2 39.2 %all-gather.13.cloned.1.call-start = ((), (), s32[]{:S(2)}) async-start(), calls=%async_computation.12 | async-start | bytes 5898240 | tf_op jit(solution)/shard_map/all_gather | solution.py:40
  9.8 72.4 %all-gather.15.cloned.1.call-start = ((), (), s32[]{:S(2)}) async-start(), calls=%async_computation.13 | async-start | bytes 5898240 | tf_op jit(solution)/shard_map/all_gather | solution.py:40
  12.4 105.8 %all-gather.17.cloned.1.call-start = ((), (), s32[]{:S(2)}) async-start(), calls=%async_computation.14 | async-start | bytes 5898240 | tf_op jit(solution)/shard_map/all_gather | solution.py:40
  13.7 140.2 %all-gather.21.cloned.1.call-start = ((), (), s32[]{:S(2)}) async-start(), calls=%async_computation.16 | async-start | bytes 5898240 | tf_op jit(solution)/shard_map/all_gather | solution.py:40
  14.3 175.3 %all-gather.23.cloned.1.call-start = ((), (), s32[]{:S(2)}) async-start(), calls=%async_computation.17 | async-start | bytes 5898240 | tf_op jit(solution)/shard_map/all_gather | solution.py:40
  15.0 210.4 %all-gather.19.cloned.1.call-start = ((), (), s32[]{:S(2)}) async-start(), calls=%async_computation.15 | async-start | bytes 5898240 | tf_op jit(solution)/shard_map/all_gather | solution.py:40
  15.6 423.8 %reduce-scatter.15.cloned.1.call-start = ((), (), s32[]{:S(2)}) async-start(), calls=%async_computation.10 | async-start | bytes 5898240 | tf_op jit(solution)/shard_map/reduce_scatter | solution.py:43
  25.2 57.0 %copy-start.19 = (f32[2048]{0:T(1024)}, f32[2048]{0:T(1024)S(1)}, u32[]{:S(2)}) copy-start(f32[2048]{0:T(1024)S(1)} %add_rsqrt_fusion) | copy-start | bytes 24580
  136.6 158.6 %copy-start.15 = (f32[2048]{0:T(1024)}, f32[2048]{0:T(1024)S(1)}, u32[]{:S(2)}) copy-start(f32[2048]{0:T(1024)S(1)} %fusion.80) | copy-start | bytes 24580
  277.7 17.5 %copy-start.18 = (f32[2048]{0:T(1024)S(1)}, f32[2048]{0:T(1024)}, u32[]{:S(2)}) copy-start(f32[2048]{0:T(1024)} %copy-done.17) | copy-start | bytes 24580
  277.7 17.6 %copy-start = (bf16[1,2048,1024]{1,2,0:T(8,128)(2,1)S(1)}, bf16[1,2048,1024]{1,2,0:T(8,128)(2,1)}, u32[]{:S(2)}) copy-start(bf16[1,2048,1024]{1,2,0:T(8,128)(2,1)} %copy.21) | copy-start | bytes 12582916
  277.7 17.6 %copy-start.5 = (bf16[2048,1024]{0,1:T(8,128)(2,1)S(1)}, bf16[2048,1024]{0,1:T(8,128)(2,1)}, u32[]{:S(2)}) copy-start(bf16[2048,1024]{0,1:T(8,128)(2,1)} %get-tuple-element.33) | copy-start | bytes 12582916
  298.8 1.9 copy-start.6
  316.7 122.7 %reduce-scatter.17.cloned.1.call-start = ((), (), s32[]{:S(2)}) async-start(), calls=%async_computation.11 | async-start | bytes 5898240 | tf_op jit(solution)/shard_map/reduce_scatter | solution.py:43
  338.7 17.2 %copy-start.20 = (f32[2048]{0:T(1024)S(1)}, f32[2048]{0:T(1024)}, u32[]{:S(2)}) copy-start(f32[2048]{0:T(1024)} %copy-done.19) | copy-start | bytes 24580
  338.7 100.7 %reduce-scatter.11.cloned.1.call-start = ((), (), s32[]{:S(2)}) async-start(), calls=%async_computation.8 | async-start | bytes 5898240 | tf_op jit(solution)/shard_map/reduce_scatter | solution.py:43
  376.2 95.7 %reduce-scatter.13.cloned.1.call-start = ((), (), s32[]{:S(2)}) async-start(), calls=%async_computation.9 | async-start | bytes 5898240 | tf_op jit(solution)/shard_map/reduce_scatter | solution.py:43
  397.2 114.0 %reduce-scatter.7.cloned.1.call-start = ((), (), s32[]{:S(2)}) async-start(), calls=%async_computation.6 | async-start | bytes 5898240 | tf_op jit(solution)/shard_map/reduce_scatter | solution.py:43
  422.4 127.7 %reduce-scatter.9.cloned.1.call-start = ((), (), s32[]{:S(2)}) async-start(), calls=%async_computation.7 | async-start | bytes 5898240 | tf_op jit(solution)/shard_map/reduce_scatter | solution.py:43
  439.3 221.6 %copy-start.2 = (bf16[2,320,1024]{2,1,0:T(8,128)(2,1)S(1)}, bf16[2,320,1024]{2,1,0:T(8,128)(2,1)}, u32[]{:S(2)}) copy-start(bf16[2,320,1024]{2,1,0:T(8,128)(2,1)} %param.15) | copy-start | bytes 3932164
  439.3 196.3 %all-reduce.3.cloned.1.call-start = ((), (), s32[]{:S(2)}) async-start(), calls=%async_computation.18 | async-start | bytes 7864320 | tf_op jit(solution)/shard_map/psum | solution.py:43
  640.8 26.4 %copy-start.13 = (bf16[1,128,2560]{2,1,0:T(8,128)(2,1)S(1)}, bf16[1,128,2560]{2,1,0:T(8,128)(2,1)}, u32[]{:S(2)}) copy-start(bf16[1,128,2560]{2,1,0:T(8,128)(2,1)} %get-tuple-element.11) | copy-start | bytes 1966084
  640.8 26.4 %copy-start.14 = (bf16[1,128,2560]{2,1,0:T(8,128)(2,1)S(1)}, bf16[1,128,2560]{2,1,0:T(8,128)(2,1)}, u32[]{:S(2)}) copy-start(bf16[1,128,2560]{2,1,0:T(8,128)(2,1)} %get-tuple-element.12) | copy-start | bytes 1966084
  660.9 6.2 copy-start.3
  660.9 6.2 copy-start.4
  660.9 6.2 copy-start.7
  661.0 7.6 %copy-start.8 = (f32[2,128,2560]{2,1,0:T(8,128)S(1)}, f32[2,128,2560]{2,1,0:T(8,128)}, u32[]{:S(2)}) copy-start(f32[2,128,2560]{2,1,0:T(8,128)} %param.16) | copy-start | bytes 7864324
  661.0 8.3 %copy-start.9 = (f32[2,128,2560]{2,1,0:T(8,128)S(1)}, f32[2,128,2560]{2,1,0:T(8,128)}, u32[]{:S(2)}) copy-start(f32[2,128,2560]{2,1,0:T(8,128)} %param.20) | copy-start | bytes 7864324
  661.0 9.0 %copy-start.10 = (f32[2,128,2560]{2,1,0:T(8,128)S(1)}, f32[2,128,2560]{2,1,0:T(8,128)}, u32[]{:S(2)}) copy-start(f32[2,128,2560]{2,1,0:T(8,128)} %param.17) | copy-start | bytes 7864324
  661.0 9.1 %copy-start.11 = (bf16[1,128,2560]{2,1,0:T(8,128)(2,1)S(1)}, bf16[1,128,2560]{2,1,0:T(8,128)(2,1)}, u32[]{:S(2)}) copy-start(bf16[1,128,2560]{2,1,0:T(8,128)(2,1)} %get-tuple-element.9) | copy-start | bytes 1966084
  661.0 9.3 %copy-start.12 = (bf16[1,128,2560]{2,1,0:T(8,128)(2,1)S(1)}, bf16[1,128,2560]{2,1,0:T(8,128)(2,1)}, u32[]{:S(2)}) copy-start(bf16[1,128,2560]{2,1,0:T(8,128)(2,1)} %get-tuple-element.10) | copy-start | bytes 1966084
  (2 other events, 1.3 us)
Sparse Core Ops, SparseCore 0:
  10.2 36.1 all-gather.12
  48.5 33.6 all-gather.14
  84.4 33.6 all-gather.16
  120.2 33.6 all-gather.20
  155.9 33.6 all-gather.22
  191.7 33.6 all-gather.18
  316.8 37.6 reduce-scatter.14
  356.8 36.8 reduce-scatter.16
  396.0 36.8 reduce-scatter.10
  435.1 36.8 reduce-scatter.12
  474.3 36.8 reduce-scatter.6
  513.3 36.8 reduce-scatter.8
  552.9 82.6 all-reduce.2
where the time goes:
time: 690 us; the launch traced here: 683 us
  matrix products  307 us (44%)
  waiting for transfers between devices  291 us (42%)
  other arithmetic  26.8 us (4%)
  local copies, waits for them, and re-layouts  25.4 us (4%)
  between operations  17.3 us (3%)
  blocking collectives  14.8 us (2%)
    reduce_scatter x6, waiting for transfers between devices, summed(): lax.psum_scatter(term, 's', scatter_dimension=0, tiled=True)  111 us
    dot_general x5, matrix products, layer(): gate = jnp.dot(a, w['w_gate'], preferred_element_type=jnp.float32)  110 us
    dot_general x5, matrix products, layer(): up = jnp.dot(a, w['w_up'], preferred_element_type=jnp.float32)  107 us
    all_gather x6, waiting for transfers between devices, fetched(): lax.all_gather(w[number], 's', axis=0, tiled=True)  92.8 us
    dot_general x5, matrix products, matmul(): jnp.dot(a, w, preferred_element_type=jnp.float32).astype(jnp.bfloat16)  89.9 us
    psum x1, waiting for transfers between devices, summed(): lax.psum(lax.psum_scatter(term, 's', scatter_dimension=0, tiled=True), 'r')  85.4 us
    unnamed x44, local copies, waits for them, and re-layouts  19.3 us
    psum x1, blocking collectives, step(): squares = lax.psum(sum((jnp.sum(g * g) for g in gradients)), 's')  14.8 us
  transfers between devices with their start and end apart: 13, of which 10 were waited for; matrix products, arithmetic and copies ran while one was open for 35% of the time, Pallas kernels for 0%

commit v1 on v0

v1 whole, which is shorter than its diff:
```python
import functools

import jax
import jax.numpy as jnp
from jax import lax
from jax.experimental import pallas as pl
from jax.experimental.pallas import tpu as pltpu
from jax.sharding import PartitionSpec as P

MESH = pl.DeviceIdType.MESH
BF16, F32 = jnp.bfloat16, jnp.float32
ANY = pl.BlockSpec(memory_space=pl.ANY)
VMEM_LIMIT = 67_000_000
RING = 4


def adamw(w, m, v, g):
    m = 0.9 * m + 0.1 * g
    v = 0.95 * v + 0.05 * g * g
    step = m * lax.rsqrt(v + 1e-8) + 0.1 * w
    return (w - 0.02 * step).astype(jnp.bfloat16), m, v


def clipped(gradients, sum_of_squares, count):
    factor = jnp.minimum(1.0, 0.5 * lax.rsqrt(sum_of_squares / count + 1e-30))
    return [g * factor for g in gradients]


def scale_of(wide):
    return lax.rsqrt(jnp.mean(wide**2, -1, keepdims=True) + 1e-6)


def dot(a, b, dims):
    return lax.dot_general(a, b, ((dims[:1], dims[1:]), ((), ())), preferred_element_type=F32)


def aligned(start, size):
    return pl.ds(pl.multiple_of(start, 16), size)


class Place:
    def __init__(self):
        s = lax.axis_index("s")
        self.x, self.c, self.y = lax.div(s, 2), lax.rem(s, 2), lax.axis_index("r")

    def chip(self, d):
        return lax.rem(self.x + d, RING)

    def row(self, d):
        return lax.rem(self.y + d, RING)

    def at_x(self, d):
        return {"s": self.chip(d) * 2 + self.c}

    def at_y(self, d):
        return {"r": self.row(d)}

    def partner(self):
        return {"s": self.x * 2 + 1 - self.c}

    def greet(self):
        barrier = pltpu.get_barrier_semaphore()
        others = [self.at_x(d) for d in (1, 2, 3)] + [self.at_y(d) for d in (1, 2, 3)] + [self.partner()]
        for other in others:
            pl.semaphore_signal(barrier, inc=1, device_id=other, device_id_type=MESH)
        pl.semaphore_wait(barrier, len(others))


def remote(src, dst, send, recv, device):
    return pltpu.make_async_remote_copy(src_ref=src, dst_ref=dst, send_sem=send, recv_sem=recv, device_id=device, device_id_type=MESH)


class Fetch:
    COPIES = 17

    def __init__(self, place, shard, whole, send, recv):
        self.p, self.shard, self.whole, self.send, self.recv = place, shard, whole, send, recv
        self.rows = shard.shape[0]
        self.mine = lax.rem(place.y, 2)

    def part(self, d, half, quarter=None, ref=None):
        n = self.rows // 2
        start = half * n
        if quarter is not None:
            n //= 2
            start = start + quarter * n
        base = 0 if ref is not None else (self.p.chip(d) * 2 + self.p.c) * self.rows
        return (self.whole if ref is None else ref).at[aligned(base + start, n), :]

    def copy(self, k):
        p, h, o = self.p, self.mine, 1 - self.mine
        own = self.whole.at[aligned((p.x * 2 + p.c) * self.rows, self.rows), :]
        right, left, up, down, partner = p.at_x(1), p.at_x(3), p.at_y(1), p.at_y(3), p.partner()
        if k < 2:
            src, dst, to = self.part(0, h, ref=self.shard), self.part(0, h), (right, left)[k]
        elif k == 2:
            src, dst, to = self.shard, own, partner
        else:
            args, to = {
                3: ((3, h), up), 4: ((3, h, 0), right), 5: ((3, h), partner),
                6: ((1, h), down), 7: ((1, h, 1), left), 8: ((1, h), partner),
                9: ((3, o), partner), 10: ((1, o), partner),
                11: ((2, h, 0), up), 12: ((2, h, 0), partner),
                13: ((2, h, 1), down), 14: ((2, h, 1), partner),
                15: ((2, o, 0), partner), 16: ((2, o, 1), partner),
            }[k]
            src = dst = self.part(*args)
        return remote(src, dst, self.send.at[k], self.recv.at[k], to)

    def start(self, *ks):
        for k in ks:
            self.copy(k).start()

    def arrived(self, *ks):
        for k in ks:
            self.copy(k).wait_recv()

    def stage(self, n):
        if n == 0:
            self.start(0, 1, 2)
        elif n == 1:
            self.arrived(0)
            self.start(4, 3, 5)
            self.arrived(1)
            self.start(7, 6, 8)
        elif n == 2:
            self.arrived(4)
            self.start(11, 12)
            self.arrived(7)
            self.start(13, 14)
            self.arrived(3)
            self.start(9)
            self.arrived(6)
            self.start(10)
        elif n == 3:
            self.arrived(11)
            self.start(15)
            self.arrived(13)
            self.start(16)
        else:
            self.arrived(2, 5, 8, 9, 10, 12, 14, 15, 16)
            for k in range(self.COPIES):
                self.copy(k).wait_send()


def first_kernel(x_ref, *refs):
    shards, outs, scratch = refs[:3], refs[3:12], refs[12:]
    g1, u1, d1, d0, a_ref, gate_ref, up_ref, hid_ref, h_ref = outs
    wg, wu, wd, stage_g, stage_u, stage_d, send, recv, local = scratch
    place = Place()
    step = pl.program_id(0)
    here = (place.x * 2 + place.c)

    def fetch(layer, m):
        whole = ((wg, wu, wd), (g1, u1, d1))[layer][m]
        return Fetch(place, shards[m].at[layer], whole, send.at[layer, m], recv.at[layer, m])

    def own0(m):
        rows = shards[m].shape[1]
        return pltpu.make_async_copy(shards[m].at[0], (wg, wu, wd)[m].at[aligned(here * rows, rows), :], local.at[m])

    def own1_in(m):
        return pltpu.make_async_copy(shards[m].at[1], (stage_g, stage_u, stage_d)[m], local.at[3 + m])

    def own1_out(m):
        rows = shards[m].shape[1]
        return pltpu.make_async_copy((stage_g, stage_u, stage_d)[m], (g1, u1, d1)[m].at[aligned(here * rows, rows), :], local.at[6 + m])

    keep_d0 = pltpu.make_async_copy(wd, d0, local.at[9])

    @pl.when(step == 0)
    def _():
        place.greet()
        for m in range(3):
            fetch(0, m).stage(0)
        for m in range(3):
            own0(m).start()
            own1_in(m).start()
        for n in range(1, 5):
            for m in range(3):
                fetch(0, m).stage(n)
            if n == 1:
                for m in range(3):
                    fetch(1, m).stage(0)
        for m in range(3):
            own0(m).wait()
            own1_in(m).wait()
            own1_out(m).start()
        keep_d0.start()

    plan = {2: [(0, 1)], 3: [(1, 1)], 5: [(2, 1), (0, 2)], 6: [(1, 2), (0, 3)], 7: [(2, 2), (1, 3)]}
    for at, todo in plan.items():

        @pl.when(step == at)
        def _(todo=todo):
            for m, n in todo:
                fetch(1, m).stage(n)

    wide = x_ref[...].astype(F32)
    a_ref[...] = (wide * scale_of(wide)).astype(BF16)
    width = wg.shape[1] // 5

    def columns(j, _):
        at = pl.ds(pl.multiple_of(j * width, 128), width)
        gate = dot(a_ref[...], wg[:, at], (1, 0))
        up = dot(a_ref[...], wu[:, at], (1, 0))
        gate_ref[:, at] = gate
        up_ref[:, at] = up
        hid_ref[:, at] = (jax.nn.silu(gate) * up).astype(BF16)
        return 0

    lax.fori_loop(0, 5, columns, 0)
    h_ref[...] = x_ref[...] + dot(hid_ref[...], wd[...], (1, 0)).astype(BF16)

    @pl.when(step == pl.num_programs(0) - 1)
    def _():
        fetch(1, 2).stage(3)
        for m in range(3):
            fetch(1, m).stage(4)
            own1_out(m).wait()
        keep_d0.wait()


def first(x, weights, tile=256):
    t, d = x.shape
    ff = weights[0].shape[2]
    gd, du, dd = ((w.shape[1], w.shape[2]) for w in weights)

    def rows(width):
        return pl.BlockSpec((tile, width), lambda i: (i, 0))

    whole = [(d, ff), (d, ff), (ff, d)]
    return pl.pallas_call(
        first_kernel,
        name="first",
        grid=(t // tile,),
        in_specs=[rows(d), ANY, ANY, ANY],
        out_specs=[ANY] * 4 + [rows(d), rows(ff), rows(ff), rows(ff), rows(d)],
        out_shape=[jax.ShapeDtypeStruct(s, BF16) for s in whole]
        + [jax.ShapeDtypeStruct((ff, d), BF16), jax.ShapeDtypeStruct((t, d), BF16)]
        + [jax.ShapeDtypeStruct((t, ff), F32)] * 2
        + [jax.ShapeDtypeStruct((t, ff), BF16), jax.ShapeDtypeStruct((t, d), BF16)],
        scratch_shapes=[pltpu.VMEM(s, BF16) for s in whole]
        + [pltpu.VMEM(s, BF16) for s in (gd, du, dd)]
        + [pltpu.SemaphoreType.DMA((2, 3, Fetch.COPIES)), pltpu.SemaphoreType.DMA((2, 3, Fetch.COPIES)), pltpu.SemaphoreType.DMA((10,))],
        compiler_params=pltpu.CompilerParams(
            collective_id=0, has_side_effects=True, vmem_limit_bytes=VMEM_LIMIT, dimension_semantics=("arbitrary",)
        ),
        cost_estimate=pl.CostEstimate(flops=6 * t * d * ff, bytes_accessed=60_000_000, transcendentals=0),
    )(x, *weights)


def middle_kernel(h_ref, dy_ref, gate0_ref, up0_ref, g1, u1, d1, d0, a_ref, hid_ref, dg1_ref, du1_ref, dh_ref, dg0_ref, du0_ref):
    wide = h_ref[...].astype(F32)
    scale = scale_of(wide)
    a_ref[...] = (wide * scale).astype(BF16)
    ff = g1.shape[1]
    width = ff // 5

    def back(by_hid, gate, up):
        sig = jax.nn.sigmoid(gate)
        silu = gate * sig
        return by_hid * up * (sig * (1.0 + gate * (1.0 - sig))), by_hid * silu, silu * up

    def layer1(j, _):
        at = pl.ds(pl.multiple_of(j * width, 128), width)
        gate = dot(a_ref[...], g1[:, at], (1, 0))
        up = dot(a_ref[...], u1[:, at], (1, 0))
        by_hid = dot(dy_ref[...], d1[at, :], (1, 1)).astype(BF16).astype(F32)
        by_gate, by_up, hid = back(by_hid, gate, up)
        hid_ref[:, at] = hid.astype(BF16)
        dg1_ref[:, at] = by_gate.astype(BF16)
        du1_ref[:, at] = by_up.astype(BF16)
        return 0

    lax.fori_loop(0, 5, layer1, 0)
    by_a = dot(dg1_ref[...], g1[...], (1, 1)).astype(BF16) + dot(du1_ref[...], u1[...], (1, 1)).astype(BF16)
    by_a = by_a.astype(F32)
    along = jnp.sum(by_a * wide, -1, keepdims=True) * (1.0 / wide.shape[-1])
    by_h = by_a * scale - wide * (scale * scale * scale * along)
    dh_ref[...] = dy_ref[...] + by_h.astype(BF16)

    def layer0(j, _):
        at = pl.ds(pl.multiple_of(j * width, 128), width)
        by_hid = dot(dh_ref[...], d0[at, :], (1, 1)).astype(BF16).astype(F32)
        by_gate, by_up, _ = back(by_hid, gate0_ref[:, at], up0_ref[:, at])
        dg0_ref[:, at] = by_gate.astype(BF16)
        du0_ref[:, at] = by_up.astype(BF16)
        return 0

    lax.fori_loop(0, 5, layer0, 0)


def middle(h, dy, gate0, up0, g1, u1, d1, d0, tile=256):
    t, d = h.shape
    ff = g1.shape[1]

    def rows(width):
        return pl.BlockSpec((tile, width), lambda i: (i, 0))

    def fixed(w):
        return pl.BlockSpec(w.shape, lambda i: (0, 0), pipeline_mode=pl.Buffered(1))

    wide, narrow = jax.ShapeDtypeStruct((t, ff), BF16), jax.ShapeDtypeStruct((t, d), BF16)
    return pl.pallas_call(
        middle_kernel,
        name="middle",
        grid=(t // tile,),
        in_specs=[rows(d), rows(d), rows(ff), rows(ff)] + [fixed(w) for w in (g1, u1, d1, d0)],
        out_specs=[rows(d), rows(ff), rows(ff), rows(ff), rows(d), rows(ff), rows(ff)],
        out_shape=[narrow, wide, wide, wide, narrow, wide, wide],
        compiler_params=pltpu.CompilerParams(vmem_limit_bytes=VMEM_LIMIT, dimension_semantics=("arbitrary",)),
        cost_estimate=pl.CostEstimate(flops=12 * t * d * ff, bytes_accessed=120_000_000, transcendentals=0),
    )(h, dy, gate0, up0, g1, u1, d1, d0)


class Sum:
    COPIES = 11

    def __init__(self, place, x_first, theirs, came, mine, r1, r2, r3, final, out, send, recv, local):
        self.p, self.x_first = place, x_first
        self.theirs, self.came, self.mine, self.r1, self.r2, self.r3 = theirs, came, mine, r1, r2, r3
        self.final, self.out, self.send, self.recv, self.local = final, out, send, recv, local
        self.width = mine.shape[3]
        self.a, self.b = (place.chip, place.row) if x_first else (place.row, place.chip)
        self.at_a, self.at_b = (place.at_x, place.at_y) if x_first else (place.at_y, place.at_x)

    def block(self, d, half=None):
        t = self.a(d)
        w = self.width // 2
        cols = slice(None) if half is None else pl.ds(half * w, w)
        return self.mine.at[t, :, :, cols] if self.x_first else self.mine.at[:, t, :, cols]

    def cell(self, d):
        return self.mine.at[self.a(0), self.b(d)] if self.x_first else self.mine.at[self.b(d), self.a(0)]

    def slot(self, d):
        rows = self.final.shape[0]
        return self.out.at[aligned(self.p.y * rows, rows), :]

    def copy(self, k):
        if k == 0:
            src, dst, to = self.theirs, self.came, self.p.partner()
        elif k < 3:
            src, dst, to = self.block(2, k - 1), self.r1.at[k - 1], self.at_a((1, 3)[k - 1])
        elif k < 5:
            src, dst, to = self.block((1, 3)[k - 3]), self.r2.at[k - 3], self.at_a((1, 3)[k - 3])
        elif k < 8:
            src, dst, to = self.cell(k - 4), self.r3.at[k - 5], self.at_b(k - 4)
        else:
            src, dst, to = self.final, self.slot(0), self.p.at_y(k - 7)
        return remote(src, dst, self.send.at[k], self.recv.at[k], to)

    def keep(self):
        return pltpu.make_async_copy(self.final, self.slot(0), self.local)

    def start(self, *ks):
        for k in ks:
            self.copy(k).start()

    def wait(self, *ks):
        for k in ks:
            self.copy(k).wait()

    def add(self, into, *terms):
        total = into[...].astype(F32)
        for term in terms:
            total = total + term[...].astype(F32)
        into[...] = total.astype(BF16)

    def stage(self, n):
        if n == 0:
            self.start(0)
        elif n == 1:
            self.wait(0)

            def one(i, _):
                self.add(self.mine.at[i], self.came.at[i])
                return 0

            lax.fori_loop(0, RING, one, 0)
            self.start(1, 2)
        elif n == 2:
            self.wait(1)
            self.add(self.block(1, 0), self.r1.at[0])
            self.start(3)
            self.wait(2)
            self.add(self.block(3, 1), self.r1.at[1])
            self.start(4)
        elif n == 3:
            self.wait(3, 4)
            self.add(self.block(0), self.r2.at[0], self.r2.at[1])
            self.start(5, 6, 7)
        elif n == 4:
            self.wait(5, 6, 7)
            total = self.cell(0)[...].astype(F32)
            for d in range(3):
                total = total + self.r3[d].astype(F32)
            self.final[...] = total.astype(BF16)
            self.start(8, 9, 10)
            self.keep().start()
        else:
            self.wait(8, 9, 10)
            self.keep().wait()


X_FIRST = (True, False, True, True, False, True)


def last_kernel(hid1, dy, a1, dg1, du1, hid0, dh, a0, dg0, du0, *refs):
    outs, scratch = refs[:6], refs[6:]
    small, wide, theirs_d, came_d, mine_d, r1_d, r2_d, r3_d, final_d = scratch[:9]
    theirs_w, came_w, mine_w, r1_w, r2_w, r3_w, final_w, send, recv, local = scratch[9:]
    place = Place()
    chunk = wide.shape[2]
    jobs = [(dy, hid1), (a1, dg1), (a1, du1), (dh, hid0), (a0, dg0), (a0, du0)]

    def load_small(m):
        return pltpu.make_async_copy(jobs[m][0], small.at[{0: 0, 1: 1, 2: 1, 3: 0, 4: 1, 5: 1}[m]], local.at[6 + m])

    def load_wide(n):
        return pltpu.make_async_copy(jobs[n // RING][1].at[:, pl.ds(n % RING * chunk, chunk)], wide.at[n % 2], local.at[12 + n % 2])

    def summed(m):
        layer, kind = m // 3, m % 3
        if kind == 0:
            bufs = theirs_d, came_d, mine_d.at[layer], r1_d.at[layer], r2_d.at[layer], r3_d.at[layer], final_d.at[layer]
        else:
            w = layer * 2 + kind - 1
            bufs = theirs_w.at[w % 2], came_w.at[w % 2], mine_w.at[w % 3], r1_w.at[w], r2_w.at[w], r3_w.at[w], final_w.at[w]
        return Sum(place, X_FIRST[m], *bufs, outs[m], send.at[m], recv.at[m], local.at[m])

    def store(m, value, x, columns):
        sums = summed(m)
        rows = value.shape[0] // 2
        first, second = value[:rows].astype(BF16), value[rows:].astype(BF16)
        low = place.c == 0
        shape = (RING, rows // RING, value.shape[1])
        sums.mine[x, :, :, columns] = jnp.where(low, first, second).reshape(shape)
        sums.theirs[x, :, :, columns] = jnp.where(low, second, first).reshape(shape)

    def compute(m, j):
        lhs = small.at[{0: 0, 1: 1, 2: 1, 3: 0, 4: 1, 5: 1}[m]]
        n = (m * RING + j) % 2
        if m % 3 == 0:
            width = lhs.shape[1] // 2

            def half(i, _):
                at = pl.ds(pl.multiple_of(i * width, 128), width)
                store(m, dot(wide[n], lhs[:, at], (0, 0)), j, at)
                return 0

            lax.fori_loop(0, 2, half, 0)
        else:
            height = lhs.shape[1] // RING

            def chip(i, _):
                at = pl.ds(pl.multiple_of(i * height, 128), height)
                store(m, dot(lhs[:, at], wide[n], (0, 0)), i, pl.ds(j * chunk, chunk))
                return 0

            lax.fori_loop(0, RING, chip, 0)

    steps = 6 * RING
    load_small(0).start()
    load_wide(0).start()
    load_small(1).start()
    place.greet()
    todo = {}
    for m in range(6):
        for n, after in enumerate((0, 2, 4, 7, 9)):
            todo.setdefault(m * RING + RING - 1 + after, []).append((m, n))
    for t in range(steps):
        m, j = divmod(t, RING)
        if j == 0 and m != 2 and m != 5:
            load_small(m).wait()
        load_wide(t).wait()
        if t + 1 < steps:
            load_wide(t + 1).start()
        if t == RING:
            load_small(3).start()
        compute(m, j)
        if t == 3 * RING - 1:
            load_small(4).start()
        for k, n in todo.pop(t, []):
            summed(k).stage(n)
    for t in sorted(todo):
        for k, n in todo[t]:
            summed(k).stage(n)
    for m in range(6):
        summed(m).stage(5)


def last(hid1, dy, a1, dg1, du1, hid0, dh, a0, dg0, du0):
    t, ff = hid1.shape
    d = dy.shape[1]
    cores = 2 * RING
    tall, flat = (ff // cores, d), (d // cores, ff)
    cells_d, cells_w = (RING, RING, tall[0] // RING, d), (RING, RING, flat[0] // RING, ff)

    def received(count, cells):
        _, _, rows, width = cells
        return [
            pltpu.VMEM((count, 2, RING, rows, width // 2), BF16),
            pltpu.VMEM((count, 2, RING, rows, width), BF16),
            pltpu.VMEM((count, 3, rows, width), BF16),
            pltpu.VMEM((count, rows, width), BF16),
        ]

    return pl.pallas_call(
        last_kernel,
        name="last",
        in_specs=[ANY] * 10,
        out_specs=[ANY] * 6,
        out_shape=[jax.ShapeDtypeStruct(s, BF16) for s in (tall, flat, flat) * 2],
        scratch_shapes=[pltpu.VMEM((2, t, d), BF16), pltpu.VMEM((2, t, ff // RING), BF16)]
        + [pltpu.VMEM(cells_d, BF16), pltpu.VMEM(cells_d, BF16), pltpu.VMEM((2, *cells_d), BF16)]
        + received(2, cells_d)
        + [pltpu.VMEM((2, *cells_w), BF16), pltpu.VMEM((2, *cells_w), BF16), pltpu.VMEM((3, *cells_w), BF16)]
        + received(4, cells_w)
        + [pltpu.SemaphoreType.DMA((6, Sum.COPIES)), pltpu.SemaphoreType.DMA((6, Sum.COPIES)), pltpu.SemaphoreType.DMA((14,))],
        compiler_params=pltpu.CompilerParams(collective_id=1, has_side_effects=True, vmem_limit_bytes=VMEM_LIMIT),
        cost_estimate=pl.CostEstimate(flops=12 * t * d * ff, bytes_accessed=90_000_000, transcendentals=0),
    )(hid1, dy, a1, dg1, du1, hid0, dh, a0, dg0, du0)


def solution(mesh):
    def step(x, dy, *arrays):
        weights, m, v = (arrays[i : i + 3] for i in (0, 3, 6))
        g1, u1, d1, d0, a0, gate0, up0, hid0, h1 = first(x[0], weights)
        a1, hid1, dg1, du1, dh, dg0, du0 = middle(h1, dy[0], gate0, up0, g1, u1, d1, d0)
        down1, gate1, up1, down0, gate_0, up_0 = last(hid1, dy[0], a1, dg1, du1, hid0, dh, a0, dg0, du0)
        gradients = [jnp.stack(pair).astype(F32) for pair in ((gate_0, gate1), (up_0, up1), (down0, down1))]
        squares = lax.psum(sum(jnp.sum(g * g) for g in gradients), "s")
        gradients = clipped(gradients, squares, lax.psum(1, "s") * sum(g.size for g in gradients))
        new = [adamw(w.astype(F32), m, v, g) for w, m, v, g in zip(weights, m, v, gradients, strict=True)]
        return tuple(one[which] for which in range(3) for one in new)

    states, cut = P(("rep", "r", "s"), None, None), P(None, "s", None)
    return jax.shard_map(
        step,
        mesh=mesh,
        in_specs=(states, states) + (cut,) * 9,
        out_specs=(P("rep", "s", None),) * 9,
        check_vma=False,
    )
```

time: 690 us -> 447 us (0.65)
  the two profiles are of different devices: /device:TPU:96 before, /device:TPU:97 now
where the time goes in v1:
time: 447 us; the launch traced here: 439 us
  Pallas kernels  399 us (89%)
  other arithmetic  19.2 us (4%)
  blocking collectives  13.9 us (3%)
    pallas_call x1, Pallas kernels, last(): pl.pallas_call(last_kernel, name='last', in_specs=[ANY] * 10, out_specs=[...  185 us
    pallas_call x1, Pallas kernels, first(): pl.pallas_call(first_kernel, name='first', grid=(t // tile,), in_specs=[r...  110 us
    pallas_call x1, Pallas kernels, middle(): pl.pallas_call(middle_kernel, name='middle', grid=(t // tile,), in_specs=...  105 us
    psum x1, blocking collectives, step(): squares = lax.psum(sum((jnp.sum(g * g) for g in gradients)), 's')  13.9 us
    convert_element_type x3, other arithmetic, adamw(): return ((w - 0.02 * step).astype(jnp.bfloat16), m, v)  13.5 us

profile of v1, /device:TPU:97, one launch (start us, length us, event | category | flops | bytes accessed | tf_op | source)
XLA Modules:
  0.0 438.6 jit_solution(7515146464056031654)
XLA Ops:
  0.6 109.7 %first.1 = (bf16[1024,2560]{1,0:T(8,128)(2,1)}, bf16[1024,2560]{1,0:T(8,128)(2,1)}, bf16[2560,1024]{1,0:T(8,128)(2,1)}, bf16[2560,1024]{1,0:T(8,128)(2,1)}, bf16...) custom-call(bf16[2048,1024]{1,0:T(8,128)(2,1)} %bitcast.20, ...), custom_call_target="tpu_custom_call" | custom-call | flops 32212254720 | bytes 60000000 | tf_op jit(solution)/shard_map/first/pallas_call | solution.py:233
  110.4 104.7 %middle.1 = (bf16[2048,1024]{1,0:T(8,128)(2,1)}, bf16[2048,2560]{1,0:T(8,128)(2,1)}, bf16[2048,2560]{1,0:T(8,128)(2,1)}, bf16[2048,2560]{1,0:T(8,128)(2,1)}, bf1...) custom-call(bf16[2048,1024]{1,0:T(8,128)(2,1)} %get-tuple-element.31.h_ref, ...), custom_call_target="tpu_custom_call" | custom-call | flops 64424509440 | bytes 120000000 | tf_op jit(solution)/shard_map/middle/pallas_call | solution.py:305
  215.0 184.6 %last.1 = (bf16[320,1024]{1,0:T(8,128)(2,1)}, bf16[128,2560]{1,0:T(8,128)(2,1)}, bf16[128,2560]{1,0:T(8,128)(2,1)}, bf16[320,1024]{1,0:T(8,128)(2,1)}, bf16[128,...) custom-call(bf16[2048,2560]{1,0:T(8,128)(2,1)} %get-tuple-element.38.hid1, bf16[2048,1024]{1,0:T(8,128)(2,1)} %bitcast.22, ...), custom_call_target="tpu_custom_call" | custom-call | flops 64424509440 | bytes 90000000 | tf_op jit(solution)/shard_map/last/pallas_call | solution.py:510
  399.7 0.0 copy-start
  399.7 0.0 copy-start.1
  399.7 0.0 copy-start.10
  399.7 2.7 fusion.11
  402.4 3.0 fusion.9
  407.3 13.9 %psum.7 = f32[]{:T(128)} all-reduce(f32[]{:T(128)S(6)} %add.51), channel_id=1, replica_groups=mesh['rep'=1,'r'=4,'s'=8] {'s'}, use_global_device_ids=true, to_apply=%region_3.0 | all-reduce | flops 1 | bytes 8 | tf_op jit(solution)/shard_map/psum | solution.py:534
  421.9 0.0 copy-done
  421.9 0.0 copy-done.1
  421.9 0.0 copy-done.10
  421.9 0.0 copy-start.4
  421.9 0.0 copy-start.5
  421.9 0.0 copy-start.6
  421.9 0.0 copy-start.7
  422.0 0.0 copy-start.11
  422.0 5.9 %fusion.17 = (bf16[2,320,1024]{2,1,0:T(8,128)(2,1)}, f32[2,320,1024]{2,1,0:T(8,128)}, f32[2,320,1024]{2,1,0:T(8,128)}) fusion(bf16[2,320,1024]{2,1,0:T(8,128)(2,1)S(1)} %copy-done.10, f32[]{:T(128)S(6)} %min_shard_map.3, bf16[1,320,1024]{2,1,0:T(8,128)(2,1)S(1)} %bitcast.9, bf16[1,320,1024]{2,1,0:T(8,128)(2,1)S(1)} %bitcast.11, f32[2,320,1024]{2,1,0:T(8,128)} %param.21, ...), kind=kLoop, calls=%fused_computation.32 | loop fusion | flops 13107200 | bytes 14417924 | tf_op jit(solution)/shard_map/convert_element_type | solution.py:21
  427.9 0.0 copy-done.4
  427.9 0.0 copy-done.5
  427.9 0.0 copy-done.6
  427.9 0.4 copy-done.7
  428.3 0.7 copy-done.11
  429.1 0.0 copy-start.2
  429.1 0.0 copy-start.12
  429.1 4.0 fusion.8
  433.1 0.0 copy-done.2
  433.1 0.0 copy-done.3
  433.1 0.0 copy-done.8
  433.1 1.2 copy-done.9
  434.3 0.3 copy-done.12
  434.6 3.5 fusion.14
  (3 shorter events, 0.0 us)
Async XLA Ops:
  399.7 22.2 %copy-start = (bf16[320,1024]{1,0:T(8,128)(2,1)S(1)}, bf16[320,1024]{1,0:T(8,128)(2,1)}, u32[]{:S(2)}) copy-start(bf16[320,1024]{1,0:T(8,128)(2,1)} %get-tuple-element.52) | copy-start | bytes 1966084
  399.7 22.2 %copy-start.1 = (bf16[320,1024]{1,0:T(8,128)(2,1)S(1)}, bf16[320,1024]{1,0:T(8,128)(2,1)}, u32[]{:S(2)}) copy-start(bf16[320,1024]{1,0:T(8,128)(2,1)} %get-tuple-element.51) | copy-start | bytes 1966084
  399.7 22.2 %copy-start.10 = (bf16[2,320,1024]{2,1,0:T(8,128)(2,1)S(1)}, bf16[2,320,1024]{2,1,0:T(8,128)(2,1)}, u32[]{:S(2)}) copy-start(bf16[2,320,1024]{2,1,0:T(8,128)(2,1)} %refs_2_.1) | copy-start | bytes 3932164
  421.9 6.0 %copy-start.4 = (bf16[128,2560]{1,0:T(8,128)(2,1)S(1)}, bf16[128,2560]{1,0:T(8,128)(2,1)}, u32[]{:S(2)}) copy-start(bf16[128,2560]{1,0:T(8,128)(2,1)} %get-tuple-element.48) | copy-start | bytes 1966084
  421.9 6.0 %copy-start.5 = (bf16[128,2560]{1,0:T(8,128)(2,1)S(1)}, bf16[128,2560]{1,0:T(8,128)(2,1)}, u32[]{:S(2)}) copy-start(bf16[128,2560]{1,0:T(8,128)(2,1)} %get-tuple-element.47) | copy-start | bytes 1966084
  421.9 6.0 %copy-start.6 = (f32[2,128,2560]{2,1,0:T(8,128)S(1)}, f32[2,128,2560]{2,1,0:T(8,128)}, u32[]{:S(2)}) copy-start(f32[2,128,2560]{2,1,0:T(8,128)} %param.19) | copy-start | bytes 7864324
  421.9 6.4 %copy-start.7 = (f32[2,128,2560]{2,1,0:T(8,128)S(1)}, f32[2,128,2560]{2,1,0:T(8,128)}, u32[]{:S(2)}) copy-start(f32[2,128,2560]{2,1,0:T(8,128)} %param.16) | copy-start | bytes 7864324
  422.0 7.1 %copy-start.11 = (bf16[2,128,2560]{2,1,0:T(8,128)(2,1)S(1)}, bf16[2,128,2560]{2,1,0:T(8,128)(2,1)}, u32[]{:S(2)}) copy-start(bf16[2,128,2560]{2,1,0:T(8,128)(2,1)} %refs_0_.1) | copy-start | bytes 3932164
  429.1 4.1 copy-start.2
  429.1 4.1 copy-start.3
  429.1 4.1 copy-start.8
  429.1 5.3 %copy-start.9 = (f32[2,128,2560]{2,1,0:T(8,128)S(1)}, f32[2,128,2560]{2,1,0:T(8,128)}, u32[]{:S(2)}) copy-start(f32[2,128,2560]{2,1,0:T(8,128)} %param.17) | copy-start | bytes 7864324
  429.1 5.6 %copy-start.12 = (bf16[2,128,2560]{2,1,0:T(8,128)(2,1)S(1)}, bf16[2,128,2560]{2,1,0:T(8,128)(2,1)}, u32[]{:S(2)}) copy-start(bf16[2,128,2560]{2,1,0:T(8,128)(2,1)} %refs_1_.1) | copy-start | bytes 3932164

commit v2 on v1

--- a/solution.py
+++ b/solution.py
@@ -11,6 +11,7 @@
 BF16, F32 = jnp.bfloat16, jnp.float32
 ANY = pl.BlockSpec(memory_space=pl.ANY)
 VMEM_LIMIT = 67_000_000
+PIECES = 10
 RING = 4
 
 
@@ -60,7 +61,7 @@
 
     def greet(self):
         barrier = pltpu.get_barrier_semaphore()
-        others = [self.at_x(d) for d in (1, 2, 3)] + [self.at_y(d) for d in (1, 2, 3)] + [self.partner()]
+        others = [self.at_x(d) for d in range(1, RING)] + [self.at_y(d) for d in range(1, RING)] + [self.partner()]
         for other in others:
             pl.semaphore_signal(barrier, inc=1, device_id=other, device_id_type=MESH)
         pl.semaphore_wait(barrier, len(others))
@@ -68,6 +69,18 @@
 
 def remote(src, dst, send, recv, device):
     return pltpu.make_async_remote_copy(src_ref=src, dst_ref=dst, send_sem=send, recv_sem=recv, device_id=device, device_id_type=MESH)
+
+
+def TABLE(h, o, right, left, up, down, partner):
+    before, beyond, far, low, high = 3, 1, 2, 0, 1
+    lower, upper, far_low, far_high = (before, h), (beyond, h), (far, h, low), (far, h, high)
+    return [
+        (lower, up), ((before, h, low), right), (lower, partner),
+        (upper, down), ((beyond, h, high), left), (upper, partner),
+        ((before, o), partner), ((beyond, o), partner),
+        (far_low, up), (far_low, partner), (far_high, down), (far_high, partner),
+        ((far, o, low), partner), ((far, o, high), partner),
+    ]
 
 
 class Fetch:
@@ -96,14 +109,7 @@
         elif k == 2:
             src, dst, to = self.shard, own, partner
         else:
-            args, to = {
-                3: ((3, h), up), 4: ((3, h, 0), right), 5: ((3, h), partner),
-                6: ((1, h), down), 7: ((1, h, 1), left), 8: ((1, h), partner),
-                9: ((3, o), partner), 10: ((1, o), partner),
-                11: ((2, h, 0), up), 12: ((2, h, 0), partner),
-                13: ((2, h, 1), down), 14: ((2, h, 1), partner),
-                15: ((2, o, 0), partner), 16: ((2, o, 1), partner),
-            }[k]
+            args, to = TABLE(h, o, right, left, up, down, partner)[k - 3]
             src = dst = self.part(*args)
         return remote(src, dst, self.send.at[k], self.recv.at[k], to)
 
@@ -138,7 +144,7 @@
             self.arrived(13)
             self.start(16)
         else:
-            self.arrived(2, 5, 8, 9, 10, 12, 14, 15, 16)
+            self.arrived(*(k for k in range(2, self.COPIES) if k not in (3, 4, 6, 7, 11, 13)))
             for k in range(self.COPIES):
                 self.copy(k).wait_send()
 
@@ -198,7 +204,7 @@
 
     wide = x_ref[...].astype(F32)
     a_ref[...] = (wide * scale_of(wide)).astype(BF16)
-    width = wg.shape[1] // 5
+    width = wg.shape[1] // PIECES
 
     def columns(j, _):
         at = pl.ds(pl.multiple_of(j * width, 128), width)
@@ -207,9 +213,9 @@
         gate_ref[:, at] = gate
         up_ref[:, at] = up
         hid_ref[:, at] = (jax.nn.silu(gate) * up).astype(BF16)
-        return 0
-
-    lax.fori_loop(0, 5, columns, 0)
+        return _
+
+    lax.fori_loop(0, PIECES, columns, 0, unroll=True)
     h_ref[...] = x_ref[...] + dot(hid_ref[...], wd[...], (1, 0)).astype(BF16)
 
     @pl.when(step == pl.num_programs(0) - 1)
@@ -255,7 +261,7 @@
     scale = scale_of(wide)
     a_ref[...] = (wide * scale).astype(BF16)
     ff = g1.shape[1]
-    width = ff // 5
+    width = ff // PIECES
 
     def back(by_hid, gate, up):
         sig = jax.nn.sigmoid(gate)
@@ -271,9 +277,9 @@
         hid_ref[:, at] = hid.astype(BF16)
         dg1_ref[:, at] = by_gate.astype(BF16)
         du1_ref[:, at] = by_up.astype(BF16)
-        return 0
-
-    lax.fori_loop(0, 5, layer1, 0)
+        return _
+
+    lax.fori_loop(0, PIECES, layer1, 0, unroll=True)
     by_a = dot(dg1_ref[...], g1[...], (1, 1)).astype(BF16) + dot(du1_ref[...], u1[...], (1, 1)).astype(BF16)
     by_a = by_a.astype(F32)
     along = jnp.sum(by_a * wide, -1, keepdims=True) * (1.0 / wide.shape[-1])
@@ -283,12 +289,12 @@
     def layer0(j, _):
         at = pl.ds(pl.multiple_of(j * width, 128), width)
         by_hid = dot(dh_ref[...], d0[at, :], (1, 1)).astype(BF16).astype(F32)
-        by_gate, by_up, _ = back(by_hid, gate0_ref[:, at], up0_ref[:, at])
+        by_gate, by_up, hid = back(by_hid, gate0_ref[:, at], up0_ref[:, at])
         dg0_ref[:, at] = by_gate.astype(BF16)
         du0_ref[:, at] = by_up.astype(BF16)
-        return 0
-
-    lax.fori_loop(0, 5, layer0, 0)
+        return _
+
+    lax.fori_loop(0, PIECES, layer0, 0, unroll=True)
 
 
 def middle(h, dy, gate0, up0, g1, u1, d1, d0, tile=256):
@@ -315,44 +321,59 @@
 
 
 class Sum:
-    COPIES = 11
-
-    def __init__(self, place, x_first, theirs, came, mine, r1, r2, r3, final, out, send, recv, local):
-        self.p, self.x_first = place, x_first
-        self.theirs, self.came, self.mine, self.r1, self.r2, self.r3 = theirs, came, mine, r1, r2, r3
-        self.final, self.out, self.send, self.recv, self.local = final, out, send, recv, local
-        self.width = mine.shape[3]
+    COPIES = 13
+
+    def __init__(self, place, x_first, start, width, theirs, came, mine, r1, r2, t1, t2, final, out, send, recv, local):
+        self.p, self.x_first, self.start_at, self.width = place, x_first, start, width
+        self.theirs, self.came, self.mine, self.out = theirs, came, mine, out
+        self.r1, self.r2, self.t1, self.t2, self.final = r1, r2, t1, t2, final
+        self.send, self.recv, self.local = send, recv, local
         self.a, self.b = (place.chip, place.row) if x_first else (place.row, place.chip)
         self.at_a, self.at_b = (place.at_x, place.at_y) if x_first else (place.at_y, place.at_x)
 
+    def columns(self, half=None):
+        w = self.width // 2
+        return pl.ds(self.start_at, self.width) if half is None else pl.ds(self.start_at + half * w, w)
+
+    def narrow(self, ref, half=False):
+        w = self.width // 2 if half else self.width
+        at = self.start_at // 2 if half else self.start_at
+        return ref.at[..., pl.ds(at, w)]
+
     def block(self, d, half=None):
-        t = self.a(d)
-        w = self.width // 2
-        cols = slice(None) if half is None else pl.ds(half * w, w)
+        t, cols = self.a(d), self.columns(half)
         return self.mine.at[t, :, :, cols] if self.x_first else self.mine.at[:, t, :, cols]
 
-    def cell(self, d):
-        return self.mine.at[self.a(0), self.b(d)] if self.x_first else self.mine.at[self.b(d), self.a(0)]
-
-    def slot(self, d):
+    def cell(self, d, half=None):
+        cols = self.columns(half)
+        return self.mine.at[self.a(0), self.b(d), :, cols] if self.x_first else self.mine.at[self.b(d), self.a(0), :, cols]
+
+    def slot(self, d, half=None):
         rows = self.final.shape[0]
-        return self.out.at[aligned(self.p.y * rows, rows), :]
+        return self.out.at[aligned(self.p.row(d) * rows, rows), self.columns(half)]
 
     def copy(self, k):
+        side = (k - 1) % 2
+        a, b, y = self.at_a((1, 3)[side]), self.at_b((1, 3)[side]), self.p.at_y((1, 3)[side])
+        near, far = (1, 3)[side], (3, 1)[side]
         if k == 0:
-            src, dst, to = self.theirs, self.came, self.p.partner()
+            src, dst, to = self.theirs.at[..., self.columns()], self.came.at[..., self.columns()], self.p.partner()
         elif k < 3:
-            src, dst, to = self.block(2, k - 1), self.r1.at[k - 1], self.at_a((1, 3)[k - 1])
+            src, dst, to = self.block(2, side), self.narrow(self.r1.at[side], True), a
         elif k < 5:
-            src, dst, to = self.block((1, 3)[k - 3]), self.r2.at[k - 3], self.at_a((1, 3)[k - 3])
-        elif k < 8:
-            src, dst, to = self.cell(k - 4), self.r3.at[k - 5], self.at_b(k - 4)
+            src, dst, to = self.block(near), self.narrow(self.r2.at[side]), a
+        elif k < 7:
+            src, dst, to = self.cell(2, side), self.narrow(self.t1.at[side], True), b
+        elif k < 9:
+            src, dst, to = self.cell(near), self.narrow(self.t2.at[side]), b
+        elif k < 11:
+            src, dst, to = self.narrow(self.final), self.slot(0), y
         else:
-            src, dst, to = self.final, self.slot(0), self.p.at_y(k - 7)
+            src, dst, to = self.slot(far, side), self.slot(far, side), y
         return remote(src, dst, self.send.at[k], self.recv.at[k], to)
 
     def keep(self):
-        return pltpu.make_async_copy(self.final, self.slot(0), self.local)
+        return pltpu.make_async_copy(self.narrow(self.final), self.slot(0), self.local)
 
     def start(self, *ks):
         for k in ks:
@@ -362,166 +383,261 @@
         for k in ks:
             self.copy(k).wait()
 
-    def add(self, into, *terms):
+    def add(self, into, *terms, to=None):
         total = into[...].astype(F32)
         for term in terms:
             total = total + term[...].astype(F32)
-        into[...] = total.astype(BF16)
-
-    def stage(self, n):
+        total = total.astype(BF16)
+        (into if to is None else to)[...] = total
+        return total
+
+    def stage(self, n, squares):
         if n == 0:
             self.start(0)
         elif n == 1:
             self.wait(0)
 
             def one(i, _):
-                self.add(self.mine.at[i], self.came.at[i])
-                return 0
+                self.add(self.mine.at[i, :, :, self.columns()], self.came.at[i, :, :, self.columns()])
+                return _
 
             lax.fori_loop(0, RING, one, 0)
             self.start(1, 2)
         elif n == 2:
             self.wait(1)
-            self.add(self.block(1, 0), self.r1.at[0])
+            self.add(self.block(1, 0), self.narrow(self.r1.at[0], True))
             self.start(3)
             self.wait(2)
-            self.add(self.block(3, 1), self.r1.at[1])
+            self.add(self.block(3, 1), self.narrow(self.r1.at[1], True))
             self.start(4)
         elif n == 3:
             self.wait(3, 4)
-            self.add(self.block(0), self.r2.at[0], self.r2.at[1])
-            self.start(5, 6, 7)
+            self.add(self.block(0), self.narrow(self.r2.at[0]), self.narrow(self.r2.at[1]))
+            self.start(5, 6)
         elif n == 4:
-            self.wait(5, 6, 7)
-            total = self.cell(0)[...].astype(F32)
-            for d in range(3):
-                total = total + self.r3[d].astype(F32)
-            self.final[...] = total.astype(BF16)
-            self.start(8, 9, 10)
+            self.wait(5, 6)
+            self.add(self.cell(1, 0), self.narrow(self.t1.at[0], True))
+            self.add(self.cell(3, 1), self.narrow(self.t1.at[1], True))
+            self.start(7, 8)
+        elif n == 5:
+            self.wait(7, 8)
+            total = self.add(self.cell(0), self.narrow(self.t2.at[0]), self.narrow(self.t2.at[1]), to=self.narrow(self.final))
+            self.start(9, 10)
             self.keep().start()
+            total = total.astype(F32)
+            squares[...] += jnp.full(squares.shape, jnp.sum(total * total), F32)
+        elif n == 6:
+            self.wait(9)
+            self.start(11)
+            self.wait(10)
+            self.start(12)
         else:
-            self.wait(8, 9, 10)
+            self.wait(11, 12)
             self.keep().wait()
 
 
-X_FIRST = (True, False, True, True, False, True)
-
-
-def last_kernel(hid1, dy, a1, dg1, du1, hid0, dh, a0, dg0, du0, *refs):
-    outs, scratch = refs[:6], refs[6:]
-    small, wide, theirs_d, came_d, mine_d, r1_d, r2_d, r3_d, final_d = scratch[:9]
-    theirs_w, came_w, mine_w, r1_w, r2_w, r3_w, final_w, send, recv, local = scratch[9:]
+class Everywhere:
+    COPIES = 7
+
+    def __init__(self, place, own, came, over_x, over_y, send, recv):
+        self.p, self.own, self.came, self.over_x, self.over_y, self.send, self.recv = place, own, came, over_x, over_y, send, recv
+
+    def copies(self, n):
+        p = self.p
+        if n == 0:
+            return [remote(self.own, self.came, self.send.at[0], self.recv.at[0], p.partner())]
+        slots, me, at = (self.over_x, p.x, p.at_x) if n == 1 else (self.over_y, p.y, p.at_y)
+        return [remote(slots.at[me], slots.at[me], self.send.at[3 * n - 3 + d], self.recv.at[3 * n - 3 + d], at(d)) for d in range(1, RING)]
+
+    def start(self, n):
+        for copy in self.copies(n):
+            copy.start()
+
+    def end(self, n):
+        for copy in self.copies(n):
+            copy.wait()
+        if n == 0:
+            self.over_x[self.p.x] = self.own[...] + self.came[...]
+            return None
+        slots = self.over_x if n == 1 else self.over_y
+        total = sum(slots[i] for i in range(RING))
+        if n == 1:
+            self.over_y[self.p.y] = total
+        return total
+
+
+TALL = (1, 3)
+UNITS = []
+for each in range(6):
+    UNITS += [(each, 0, 1, True)] if each in TALL else [(each, share, 2, share > 0) for share in range(2)]
+AFTER = (0, 2, 4, *range(7, 14, 2))
+
+
+def last_kernel(a1, dg1, dy, hid1, du1, dh, hid0, a0, dg0, du0, *refs):
+    outs, sum_ref, scratch = refs[:6], refs[6], refs[7:]
+    small, wide = scratch[:2]
+    bufs_d, bufs_w = scratch[2:10], scratch[10:18]
+    own, own_came, over_x, over_y, send, recv, local, every_send, every_recv = scratch[18:]
     place = Place()
     chunk = wide.shape[2]
-    jobs = [(dy, hid1), (a1, dg1), (a1, du1), (dh, hid0), (a0, dg0), (a0, du0)]
+    wides = (dg1, hid1, du1, hid0, dg0, du0)
+    smalls = {0: (a1, 0), 1: (dy, 1), 3: (dh, 1), 4: (a0, 0)}
 
     def load_small(m):
-        return pltpu.make_async_copy(jobs[m][0], small.at[{0: 0, 1: 1, 2: 1, 3: 0, 4: 1, 5: 1}[m]], local.at[6 + m])
-
-    def load_wide(n):
-        return pltpu.make_async_copy(jobs[n // RING][1].at[:, pl.ds(n % RING * chunk, chunk)], wide.at[n % 2], local.at[12 + n % 2])
-
-    def summed(m):
-        layer, kind = m // 3, m % 3
-        if kind == 0:
-            bufs = theirs_d, came_d, mine_d.at[layer], r1_d.at[layer], r2_d.at[layer], r3_d.at[layer], final_d.at[layer]
-        else:
-            w = layer * 2 + kind - 1
-            bufs = theirs_w.at[w % 2], came_w.at[w % 2], mine_w.at[w % 3], r1_w.at[w], r2_w.at[w], r3_w.at[w], final_w.at[w]
-        return Sum(place, X_FIRST[m], *bufs, outs[m], send.at[m], recv.at[m], local.at[m])
-
-    def store(m, value, x, columns):
-        sums = summed(m)
+        src, slot = smalls[m]
+        return pltpu.make_async_copy(src, small.at[slot], local.at[m])
+
+    def load_wide(m, t):
+        slot = lax.rem(t, 2)
+        at = pl.ds(pl.multiple_of(lax.rem(t, RING) * chunk, 128), chunk)
+        return pltpu.make_async_copy(wides[m].at[:, at], wide.at[slot], local.at[6 + slot])
+
+    def tall_buffers(layer):
+        return [buf.at[pick] for buf, pick in zip(bufs_d, (0, 0) + (layer,) * 6, strict=True)]
+
+    def flat_buffers(m):
+        w = (m + 1) // 2
+        return [buf.at[pick] for buf, pick in zip(bufs_w, (w % 2, w % 2) + (w,) * 6, strict=True)]
+
+    def unit(k):
+        m, share, shares, x_first = UNITS[k]
+        bufs = tall_buffers(m // 3) if m in TALL else flat_buffers(m)
+        width = bufs[2].shape[3] // shares
+        return Sum(place, x_first, share * width, width, *bufs, outs[m], send.at[k], recv.at[k], local.at[8 + k])
+
+    def store(bufs, value, x, columns):
+        theirs, _, mine = bufs[:3]
         rows = value.shape[0] // 2
         first, second = value[:rows].astype(BF16), value[rows:].astype(BF16)
         low = place.c == 0
         shape = (RING, rows // RING, value.shape[1])
-        sums.mine[x, :, :, columns] = jnp.where(low, first, second).reshape(shape)
-        sums.theirs[x, :, :, columns] = jnp.where(low, second, first).reshape(shape)
-
-    def compute(m, j):
-        lhs = small.at[{0: 0, 1: 1, 2: 1, 3: 0, 4: 1, 5: 1}[m]]
-        n = (m * RING + j) % 2
-        if m % 3 == 0:
-            width = lhs.shape[1] // 2
-
-            def half(i, _):
-                at = pl.ds(pl.multiple_of(i * width, 128), width)
-                store(m, dot(wide[n], lhs[:, at], (0, 0)), j, at)
-                return 0
-
-            lax.fori_loop(0, 2, half, 0)
-        else:
-            height = lhs.shape[1] // RING
-
-            def chip(i, _):
-                at = pl.ds(pl.multiple_of(i * height, 128), height)
-                store(m, dot(lhs[:, at], wide[n], (0, 0)), i, pl.ds(j * chunk, chunk))
-                return 0
-
-            lax.fori_loop(0, RING, chip, 0)
+        mine[x, :, :, columns] = jnp.where(low, first, second).reshape(shape)
+        theirs[x, :, :, columns] = jnp.where(low, second, first).reshape(shape)
+
+    def tall(m, j, slot):
+        lhs, bufs = small.at[1], tall_buffers(m // 3)
+        width = lhs.shape[1] // 2
+        for i in range(2):
+            at = pl.ds(i * width, width)
+            store(bufs, dot(wide[slot], lhs[:, at], (0, 0)), j, at)
+
+    def flat(m, j, slot):
+        lhs, bufs = small.at[0], flat_buffers(m)
+        height = lhs.shape[1] // RING
+        columns = pl.ds(pl.multiple_of(j * chunk, 128), chunk)
+        for i in range(RING):
+            store(bufs, dot(lhs[:, i * height : (i + 1) * height], wide[slot], (0, 0)), i, columns)
 
     steps = 6 * RING
     load_small(0).start()
-    load_wide(0).start()
+    load_wide(0, 0).start()
     load_small(1).start()
+    own[...] = jnp.zeros_like(own)
     place.greet()
     todo = {}
-    for m in range(6):
-        for n, after in enumerate((0, 2, 4, 7, 9)):
-            todo.setdefault(m * RING + RING - 1 + after, []).append((m, n))
-    for t in range(steps):
-        m, j = divmod(t, RING)
-        if j == 0 and m != 2 and m != 5:
-            load_small(m).wait()
-        load_wide(t).wait()
-        if t + 1 < steps:
-            load_wide(t + 1).start()
-        if t == RING:
-            load_small(3).start()
-        compute(m, j)
-        if t == 3 * RING - 1:
-            load_small(4).start()
-        for k, n in todo.pop(t, []):
-            summed(k).stage(n)
-    for t in sorted(todo):
-        for k, n in todo[t]:
-            summed(k).stage(n)
-    for m in range(6):
-        summed(m).stage(5)
-
-
-def last(hid1, dy, a1, dg1, du1, hid0, dh, a0, dg0, du0):
-    t, ff = hid1.shape
-    d = dy.shape[1]
+    for k, (m, share, shares, _) in enumerate(UNITS):
+        ready = m * RING + (RING * (share + 1)) // shares - 1
+        for n, after in enumerate(AFTER):
+            todo.setdefault(ready + after, []).append((k, n))
+
+    def work(t, carry):
+        m, j, slot = t // RING, t % RING, t % 2
+        for first in smalls:
+
+            @pl.when(t == first * RING)
+            def _(first=first):
+                load_small(first).wait()
+
+        load_wide(0, t).wait()
+        for each in range(6):
+
+            @pl.when((t + 1) // RING == each)
+            def _(each=each):
+                load_wide(each, t + 1).start()
+
+        for each, free in ((3, 2), (4, 3)):
+
+            @pl.when(t == free * RING)
+            def _(each=each):
+                load_small(each).start()
+
+        is_tall = (m == TALL[0]) | (m == TALL[1])
+
+        @pl.when(is_tall)
+        def _():
+            tall(m, j, slot)
+
+        @pl.when(jnp.logical_not(is_tall))
+        def _():
+            flat(m, j, slot)
+
+        for at in sorted(todo):
+            if at < steps:
+
+                @pl.when(t == at)
+                def _(at=at):
+                    for k, n in todo[at]:
+                        unit(k).stage(n, own)
+
+        return carry
+
+    lax.fori_loop(0, steps, work, 0)
+    rest = [each for t in sorted(todo) if t >= steps for each in todo[t]]
+    for k, n in rest:
+        if n < 6:
+            unit(k).stage(n, own)
+    every = Everywhere(place, own, own_came, over_x, over_y, every_send, every_recv)
+    every.start(0)
+    for k, n in rest:
+        if n == 6:
+            unit(k).stage(n, own)
+    every.end(0)
+    every.start(1)
+    every.end(1)
+    every.start(2)
+    for k in range(len(UNITS)):
+        unit(k).stage(7, own)
+    sum_ref[...] = every.end(2)
+
+
+def last(*operands):
+    a1, dg1 = operands[:2]
+    t, d = a1.shape
+    ff = dg1.shape[1]
     cores = 2 * RING
     tall, flat = (ff // cores, d), (d // cores, ff)
     cells_d, cells_w = (RING, RING, tall[0] // RING, d), (RING, RING, flat[0] // RING, ff)
 
-    def received(count, cells):
+    def buffers(theirs, mine, count, cells):
         _, _, rows, width = cells
         return [
+            pltpu.VMEM((theirs, *cells), BF16),
+            pltpu.VMEM((theirs, *cells), BF16),
+            pltpu.VMEM((mine, *cells), BF16),
             pltpu.VMEM((count, 2, RING, rows, width // 2), BF16),
             pltpu.VMEM((count, 2, RING, rows, width), BF16),
-            pltpu.VMEM((count, 3, rows, width), BF16),
+            pltpu.VMEM((count, 2, rows, width // 2), BF16),
+            pltpu.VMEM((count, 2, rows, width), BF16),
             pltpu.VMEM((count, rows, width), BF16),
         ]
 
+    units = len(UNITS)
+    number = (8, 128)
     return pl.pallas_call(
         last_kernel,
         name="last",
         in_specs=[ANY] * 10,
-        out_specs=[ANY] * 6,
-        out_shape=[jax.ShapeDtypeStruct(s, BF16) for s in (tall, flat, flat) * 2],
+        out_specs=[ANY] * 6 + [pl.BlockSpec(memory_space=pltpu.VMEM)],
+        out_shape=[jax.ShapeDtypeStruct(s, BF16) for s in (flat, tall, flat, tall, flat, flat)] + [jax.ShapeDtypeStruct(number, F32)],
         scratch_shapes=[pltpu.VMEM((2, t, d), BF16), pltpu.VMEM((2, t, ff // RING), BF16)]
-        + [pltpu.VMEM(cells_d, BF16), pltpu.VMEM(cells_d, BF16), pltpu.VMEM((2, *cells_d), BF16)]
-        + received(2, cells_d)
-        + [pltpu.VMEM((2, *cells_w), BF16), pltpu.VMEM((2, *cells_w), BF16), pltpu.VMEM((3, *cells_w), BF16)]
-        + received(4, cells_w)
-        + [pltpu.SemaphoreType.DMA((6, Sum.COPIES)), pltpu.SemaphoreType.DMA((6, Sum.COPIES)), pltpu.SemaphoreType.DMA((14,))],
+        + buffers(1, 2, 2, cells_d)
+        + buffers(2, 4, 4, cells_w)
+        + [pltpu.VMEM(number, F32), pltpu.VMEM(number, F32), pltpu.VMEM((RING, *number), F32), pltpu.VMEM((RING, *number), F32)]
+        + [pltpu.SemaphoreType.DMA((units, Sum.COPIES)), pltpu.SemaphoreType.DMA((units, Sum.COPIES)), pltpu.SemaphoreType.DMA((8 + units,))]
+        + [pltpu.SemaphoreType.DMA((Everywhere.COPIES,)), pltpu.SemaphoreType.DMA((Everywhere.COPIES,))],
         compiler_params=pltpu.CompilerParams(collective_id=1, has_side_effects=True, vmem_limit_bytes=VMEM_LIMIT),
         cost_estimate=pl.CostEstimate(flops=12 * t * d * ff, bytes_accessed=90_000_000, transcendentals=0),
-    )(hid1, dy, a1, dg1, du1, hid0, dh, a0, dg0, du0)
+    )(*operands)
 
 
 def solution(mesh):
@@ -529,10 +645,9 @@
         weights, m, v = (arrays[i : i + 3] for i in (0, 3, 6))
         g1, u1, d1, d0, a0, gate0, up0, hid0, h1 = first(x[0], weights)
         a1, hid1, dg1, du1, dh, dg0, du0 = middle(h1, dy[0], gate0, up0, g1, u1, d1, d0)
-        down1, gate1, up1, down0, gate_0, up_0 = last(hid1, dy[0], a1, dg1, du1, hid0, dh, a0, dg0, du0)
+        gate1, down1, up1, down0, gate_0, up_0, squares = last(a1, dg1, dy[0], hid1, du1, dh, hid0, a0, dg0, du0)
         gradients = [jnp.stack(pair).astype(F32) for pair in ((gate_0, gate1), (up_0, up1), (down0, down1))]
-        squares = lax.psum(sum(jnp.sum(g * g) for g in gradients), "s")
-        gradients = clipped(gradients, squares, lax.psum(1, "s") * sum(g.size for g in gradients))
+        gradients = clipped(gradients, squares[0, 0], lax.psum(1, "s") * sum(g.size for g in gradients))
         new = [adamw(w.astype(F32), m, v, g) for w, m, v, g in zip(weights, m, v, gradients, strict=True)]
         return tuple(one[which] for which in range(3) for one in new)
 

time: 447 us -> 368 us (0.82)
  the two profiles are of different devices: /device:TPU:97 before, /device:TPU:96 now
where the time goes in v2:
time: 368 us
  Pallas kernels  348 us (95%)
  other arithmetic  13.6 us (4%)
  local copies, waits for them, and re-layouts  4.51 us (1%)
    pallas_call x1, Pallas kernels, last(): pl.pallas_call(last_kernel, name='last', in_specs=[ANY] * 10, out_specs=[...  157 us
    pallas_call x1, Pallas kernels, first(): pl.pallas_call(first_kernel, name='first', grid=(t // tile,), in_specs=[r...  103 us
    pallas_call x1, Pallas kernels, middle(): pl.pallas_call(middle_kernel, name='middle', grid=(t // tile,), in_specs=...  88.6 us
    convert_element_type x2, other arithmetic, adamw(): return ((w - 0.02 * step).astype(jnp.bfloat16), m, v)  13.6 us

profile of v2, /device:TPU:96, one launch (start us, length us, event | category | flops | bytes accessed | tf_op | source)
XLA Modules:
  0.0 368.0 jit_solution(15287298734814802513)
XLA Ops:
  0.6 102.8 %first.1 = (bf16[1024,2560]{1,0:T(8,128)(2,1)}, bf16[1024,2560]{1,0:T(8,128)(2,1)}, bf16[2560,1024]{1,0:T(8,128)(2,1)}, bf16[2560,1024]{1,0:T(8,128)(2,1)}, bf16...) custom-call(bf16[2048,1024]{1,0:T(8,128)(2,1)} %bitcast.15, ...), custom_call_target="tpu_custom_call" | custom-call | flops 32212254720 | bytes 60000000 | tf_op jit(solution)/shard_map/first/pallas_call | solution.py:239
  103.4 88.6 %middle.1 = (bf16[2048,1024]{1,0:T(8,128)(2,1)}, bf16[2048,2560]{1,0:T(8,128)(2,1)}, bf16[2048,2560]{1,0:T(8,128)(2,1)}, bf16[2048,2560]{1,0:T(8,128)(2,1)}, bf1...) custom-call(bf16[2048,1024]{1,0:T(8,128)(2,1)} %get-tuple-element.32.h_ref, ...), custom_call_target="tpu_custom_call" | custom-call | flops 64424509440 | bytes 120000000 | tf_op jit(solution)/shard_map/middle/pallas_call | solution.py:311
  192.0 157.1 %last.1 = (bf16[128,2560]{1,0:T(8,128)(2,1)}, bf16[320,1024]{1,0:T(8,128)(2,1)}, bf16[128,2560]{1,0:T(8,128)(2,1)}, bf16[320,1024]{1,0:T(8,128)(2,1)}, bf16[128,...) custom-call(bf16[2048,1024]{1,0:T(8,128)(2,1)} %get-tuple-element.39.a1, ...), custom_call_target="tpu_custom_call" | custom-call | flops 64424509440 | bytes 90000000 | tf_op jit(solution)/shard_map/last/pallas_call | solution.py:626
  349.2 1.2 slice.3
  351.0 0.0 copy-start
  351.1 0.0 copy-start.1
  351.1 0.0 copy-start.2
  351.1 0.0 copy-start.3
  351.1 0.0 copy-start.4
  351.1 0.0 copy-start.5
  351.1 0.0 copy-start.6
  351.1 0.0 copy-start.7
  351.1 6.3 %fusion.8 = (bf16[2,320,1024]{2,1,0:T(8,128)(2,1)}, f32[2,320,1024]{2,1,0:T(8,128)}, f32[2,320,1024]{2,1,0:T(8,128)}) fusion(bf16[2,320,1024]{2,1,0:T(8,128)(2,1)} %refs_2_.1, f32[]{:T(128)} %bitcast.4, bf16[1,320,1024]{2,1,0:T(8,128)(2,1)} %bitcast.9, bf16[1,320,1024]{2,1,0:T(8,128)(2,1)} %bitcast.10, f32[2,320,1024]{2,1,0:T(8,128)} %param.21, ...), kind=kLoop, calls=%fused_computation.17 | loop fusion | flops 13107200 | bytes 14417924 | tf_op jit(solution)/shard_map/convert_element_type | solution.py:22
  357.5 0.0 copy-done
  357.5 0.2 copy-done.1
  357.7 1.3 copy-done.2
  359.0 0.7 copy-done.3
  359.8 0.3 copy-done.4
  360.1 0.4 copy-done.5
  360.4 0.1 copy-done.6
  360.6 0.2 copy-done.7
  360.8 7.3 %fusion.2 = (bf16[2,128,2560]{2,1,0:T(8,128)(2,1)}, f32[2,128,2560]{2,1,0:T(8,128)}, f32[2,128,2560]{2,1,0:T(8,128)}, bf16[2,128,2560]{2,1,0:T(8,128)(2,1)}, f32...) fusion(bf16[2,128,2560]{2,1,0:T(8,128)(2,1)S(1)} %copy-done.4, f32[]{:T(128)} %bitcast.4, ...), kind=kLoop, calls=%fused_computation.11 | loop fusion | flops 26214400 | bytes 28835844 | tf_op jit(solution)/shard_map/convert_element_type | solution.py:22
Async XLA Ops:
  351.0 6.4 %copy-start = (f32[2,128,2560]{2,1,0:T(8,128)S(1)}, f32[2,128,2560]{2,1,0:T(8,128)}, u32[]{:S(2)}) copy-start(f32[2,128,2560]{2,1,0:T(8,128)} %param.19) | copy-start | bytes 7864324
  351.1 6.6 %copy-start.1 = (f32[2,128,2560]{2,1,0:T(8,128)S(1)}, f32[2,128,2560]{2,1,0:T(8,128)}, u32[]{:S(2)}) copy-start(f32[2,128,2560]{2,1,0:T(8,128)} %param.16) | copy-start | bytes 7864324
  351.1 7.9 %copy-start.2 = (f32[2,128,2560]{2,1,0:T(8,128)S(1)}, f32[2,128,2560]{2,1,0:T(8,128)}, u32[]{:S(2)}) copy-start(f32[2,128,2560]{2,1,0:T(8,128)} %param.20) | copy-start | bytes 7864324
  351.1 8.7 %copy-start.3 = (f32[2,128,2560]{2,1,0:T(8,128)S(1)}, f32[2,128,2560]{2,1,0:T(8,128)}, u32[]{:S(2)}) copy-start(f32[2,128,2560]{2,1,0:T(8,128)} %param.17) | copy-start | bytes 7864324
  351.1 9.0 %copy-start.4 = (bf16[2,128,2560]{2,1,0:T(8,128)(2,1)S(1)}, bf16[2,128,2560]{2,1,0:T(8,128)(2,1)}, u32[]{:S(2)}) copy-start(bf16[2,128,2560]{2,1,0:T(8,128)(2,1)} %refs_0_.1) | copy-start | bytes 3932164
  351.1 9.3 %copy-start.5 = (bf16[2,128,2560]{2,1,0:T(8,128)(2,1)S(1)}, bf16[2,128,2560]{2,1,0:T(8,128)(2,1)}, u32[]{:S(2)}) copy-start(bf16[2,128,2560]{2,1,0:T(8,128)(2,1)} %refs_1_.1) | copy-start | bytes 3932164
  351.1 9.5 %copy-start.6 = (bf16[128,2560]{1,0:T(8,128)(2,1)S(1)}, bf16[128,2560]{1,0:T(8,128)(2,1)}, u32[]{:S(2)}) copy-start(bf16[128,2560]{1,0:T(8,128)(2,1)} %get-tuple-element.49) | copy-start | bytes 1966084
  351.1 9.6 %copy-start.7 = (bf16[128,2560]{1,0:T(8,128)(2,1)S(1)}, bf16[128,2560]{1,0:T(8,128)(2,1)}, u32[]{:S(2)}) copy-start(bf16[128,2560]{1,0:T(8,128)(2,1)} %get-tuple-element.52) | copy-start | bytes 1966084
